TPU v7x, 32 devices: a whole 2x2x4 slice. The times are simulated.
32 devices in a mesh: dp: 8 (over z, x), cand: 4 (over y, core).
Axes of the slice: x: 2, y: 2, z: 4, core: 2. Of those that a mesh axis runs over, the one named last changes fastest.
Arguments:
- hidden: bfloat16 [16, 32, 128, 768], P('dp', 'cand'), may hold values from -24 to 24
- attn_weight: bfloat16 [768, 3072], P('dp'), may hold values from -1 to 1
- norm_gain: float32 [768], replicated, may hold values from 0.2 to 4
- pos_bias: float32 [12, 128, 128], replicated, may hold values from -5 to 5
- score_weight: float32 [768], replicated, may hold values from -4 to 4
- pair_lengths: int32 [16, 32], P('dp', 'cand'), may hold values from 32 to 128
- labels: int32 [16, 32], P('dp', 'cand'), may hold values from 0 to 3
Outputs:
- update: float32 [768, 3072], P('dp')
- loss: float32 [16], P('dp')
All inputs are finite; a program needn't handle non-finite values.
Results may differ from a plain program's by a relative error of at most 0.017.
Values may be sent and summed in bfloat16 or wider, within the bound.
No kernel may reach another device: no remote copies, remote signals or barrier semaphores. Data moves between devices by JAX's collectives and lax.ppermute only.
A program may use at most 128 MiB of HBM per device.

v0:
```python
import jax
import jax.numpy as jnp
from jax import lax
from jax.sharding import PartitionSpec as P

EPS = 1e-06


def rms_rows(values, gain):
    factor = lax.rsqrt(jnp.mean(values * values, axis=-1, keepdims=True) + EPS)
    return values * factor * gain


def attend(qkv, pos_bias, pair_len):
    batch, seq, triple = qkv.shape
    width = triple // 3
    heads = pos_bias.shape[0]
    head_size = width // heads
    parts = qkv.reshape(batch, seq, 3, heads, head_size)
    logits = jnp.einsum(
        "bqhd,bkhd->bhqk", parts[:, :, 0], parts[:, :, 1], preferred_element_type=jnp.float32
    )
    logits = logits + pos_bias[None]
    valid = jnp.arange(seq, dtype=jnp.int32)[None, :] < pair_len[:, None]
    logits = jnp.where(valid[:, None, None, :], logits, -1e30)
    highest = jnp.max(logits, axis=-1, keepdims=True)
    expo = jnp.exp(logits - highest)
    probs = (expo / jnp.sum(expo, axis=-1, keepdims=True)).astype(jnp.bfloat16)
    context = jnp.einsum(
        "bhqk,bkhd->bqhd", probs, parts[:, :, 2], preferred_element_type=jnp.float32
    )
    return context.astype(jnp.bfloat16).reshape(batch, seq, width)


def score_head(pooled, score_weight):
    return jnp.sum(rms_rows(pooled, 1.0) * score_weight, axis=-1)


def shards(hidden, attn_weight, norm_gain, pos_bias, score_weight, pair_lengths, labels):
    q_local, c_local, seq, width = hidden.shape
    weights = lax.all_gather(attn_weight, "dp", axis=0, tiled=True)
    tokens = hidden.reshape(q_local * c_local, seq, width)
    pair_len = pair_lengths.reshape(-1)
    values = tokens.astype(jnp.float32)
    normed = rms_rows(values, norm_gain).astype(jnp.bfloat16)
    flat_norm = normed.reshape(-1, width)
    qkv = jnp.dot(flat_norm, weights[:, : 3 * width], preferred_element_type=jnp.float32)
    qkv = qkv.astype(jnp.bfloat16).reshape(q_local * c_local, seq, 3 * width)
    context, attend_back = jax.vjp(lambda block: attend(block, pos_bias, pair_len), qkv)
    flat_ctx = context.reshape(-1, width)
    out_rows = values + jnp.dot(
        flat_ctx, weights[:, 3 * width :], preferred_element_type=jnp.float32
    ).reshape(values.shape)
    live = (jnp.arange(seq, dtype=jnp.int32)[None, :] < pair_len[:, None]).astype(jnp.float32)
    share = live / pair_len.astype(jnp.float32)[:, None]
    pooled = jnp.sum(out_rows * share[:, :, None], axis=1)
    flat_scores, head_back = jax.vjp(lambda vector: score_head(vector, score_weight), pooled)
    scores = flat_scores.reshape(q_local, c_local)
    target = jnp.exp(labels.astype(jnp.float32))
    highest = lax.pmax(jnp.max(scores, axis=1), "cand")
    expsum, target_sum, target_dot = lax.psum(
        (
            jnp.sum(jnp.exp(scores - highest[:, None]), axis=1),
            jnp.sum(target, axis=1),
            jnp.sum(target * scores, axis=1),
        ),
        "cand",
    )
    loss = highest + jnp.log(expsum) - target_dot / target_sum
    score_grad = jnp.exp(scores - highest[:, None]) / expsum[:, None] - target / target_sum[:, None]
    pooled_grad = head_back(score_grad.reshape(-1))[0]
    out_grad = (pooled_grad[:, None, :] * share[:, :, None]).astype(jnp.bfloat16)
    flat_out = out_grad.reshape(-1, width)
    context_grad = jnp.dot(flat_out, weights[:, 3 * width :].T, preferred_element_type=jnp.float32)
    context_grad = context_grad.astype(jnp.bfloat16).reshape(context.shape)
    qkv_grad = attend_back(context_grad)[0].reshape(-1, 3 * width)
    dims = (((0,), (0,)), ((), ()))
    first = lax.dot_general(flat_norm, qkv_grad, dims, preferred_element_type=jnp.float32)
    second = lax.dot_general(flat_ctx, flat_out, dims, preferred_element_type=jnp.float32)
    shard = lax.psum_scatter(
        jnp.concatenate([first, second], axis=1).astype(jnp.bfloat16),
        "dp",
        scatter_dimension=0,
        tiled=True,
    ).astype(jnp.float32)
    shard = lax.psum(shard.astype(jnp.bfloat16), "cand").astype(jnp.float32)
    squares = lax.psum(jnp.sum(shard * shard), "dp")
    rms_value = jnp.sqrt(squares / (4.0 * width * width))
    update = shard / (rms_value + EPS)
    return (update, loss)


def solution(mesh):
    in_specs = (
        P("dp", "cand", None, None),
        P("dp", None),
        P(),
        P(),
        P(),
        P("dp", "cand"),
        P("dp", "cand"),
    )
    out_specs = (P("dp", None), P("dp"))
    return jax.shard_map(shards, mesh=mesh, in_specs=in_specs, out_specs=out_specs, check_vma=False)
```

profile of v0, /device:TPU:0, one launch (start us, length us, event | category | flops | bytes accessed | tf_op | source)
XLA Modules:
  0.0 460.7 jit_solution(10536083495842605806)
XLA Ops:
  18.8 73.4 %all-gather.2.cloned.1.call-done = bf16[768,3072]{1,0:T(8,128)(2,1)} async-done(((bf16[96,3072]{1,0:T(8,128)(2,1)}), bf16[768,3072]{1,0:T(8,128)(2,1)}) %all-gather.2.cloned.1.call-update) | async-done | bytes 4718608 | tf_op jit(solution)/shard_map/all_gather | solution.py:41
  92.3 12.5 %convolution_convert_fusion = bf16[2048,2304]{1,0:T(8,128)(2,1)} fusion(bf16[2048,768]{1,0:T(8,128)(2,1)} %fusion.13, bf16[768,3072]{1,0:T(8,128)(2,1)} %all-gather.2.cloned.1.call-done), kind=kOutput, calls=%fused_computation.11 | convolution fusion | flops 7252475904 | bytes 16121856 | tf_op jit(solution)/shard_map/dot_general | solution.py:47
  104.8 12.7 %copy.20 = bf16[2048,2304]{0,1:T(8,128)(2,1)} copy(bf16[2048,2304]{1,0:T(8,128)(2,1)} %convolution_convert_fusion) | data formatting | bytes 18874368 | tf_op jit(solution)/shard_map/convert_element_type | solution.py:48
  117.5 10.9 %copy.45 = bf16[288,8,16,128]{3,2,1,0:T(8,128)(2,1)} copy(bf16[288,8,16,128]{3,1,2,0:T(8,128)(2,1)} %bitcast.104) | data formatting | bytes 18874368
  128.4 6.4 %fusion.56 = (bf16[16,128,1,12,64]{1,0,4,3,2:T(8,128)(2,1)}, bf16[16,128,1,12,64]{1,0,4,3,2:T(8,128)(2,1)}, bf16[16,128,1,12,64]{1,0,4,3,2:T(8,128)(2,1)S(1)}) fusion(bf16[16,128,3,12,64]{1,0,4,3,2:T(8,128)(2,1)} %bitcast.103), kind=kLoop, calls=%fused_computation.91 | loop fusion | bytes 18874368 | tf_op jit(solution)/shard_map/jvp()/slice | solution.py:30
  134.8 7.5 %fusion.5 = (f32[16,12,128]{2,1,0:T(8,128)S(1)}, f32[16,12,128,128]{2,3,1,0:T(8,128)S(1)}) fusion(f32[12,128,128]{1,2,0:T(8,128)S(1)} %copy-done.11, pred[16,128]{1,0:T(8,128)(4,1)S(1)} %iota_compare_fusion, bf16[16,128,1,12,64]{1,0,4,3,2:T(8,128)(2,1)S(1)} %get-tuple-element.15, bf16[16,128,1,12,64]{1,0,4,3,2:T(8,128)(2,1)} %get-tuple-element.14), kind=kOutput, calls=%fused_computation.13 | convolution fusion | flops 412065792 | bytes 19761152 | tf_op jit(solution)/shard_map/jvp(bqhd,bkhd->bhqk)/dot_general | solution.py:20
  142.3 3.4 fusion.37
  146.9 8.1 %convert_reduce_fusion = (f32[16,12,128]{2,1,0:T(8,128)S(1)}, pred[16,12,128,128]{2,3,1,0:T(32,128)(4,1)}, bf16[16,12,128,128]{2,3,1,0:T(8,128)(2,1)S(1)}) fusion(f32[16,12,128]{2,1,0:T(8,128)S(1)} %get-tuple-element.20, f32[16,12,128,128]{2,3,1,0:T(8,128)S(1)} %get-tuple-element.21, f32[12,128,128]{1,2,0:T(8,128)S(1)} %copy-done.11, ...), kind=kLoop, calls=%fused_computation.7 | loop fusion | flops 25141248 | bytes 23103488 | tf_op jit(solution)/shard_map/jvp()/reduce_sum | solution.py:26
  159.2 4.6 fusion.15
  164.3 5.7 %pmax.7 = f32[2]{0:T(128)S(1)} all-reduce(f32[2]{0:T(128)S(1)} %reduce_max.19), channel_id=1, replica_groups=mesh['dp'=8,'cand'=4] {'cand'}, use_global_device_ids=true, to_apply=%region_7.8 | all-reduce | flops 2 | bytes 16 | tf_op jit(solution)/shard_map/pmax | solution.py:60
  170.2 6.6 %all-reduce.3 = (f32[2]{0:T(128)S(1)}, f32[2]{0:T(128)S(1)}, f32[2]{0:T(128)S(1)}) all-reduce(f32[2]{0:T(128)S(1)} %get-tuple-element.3, f32[2]{0:T(128)S(1)} %get-tuple-element.4, f32[2]{0:T(128)S(1)} %get-tuple-element.2), channel_id=1, replica_groups=mesh['dp'=8,'cand'=4] {'cand'}, use_global_device_ids=true, to_apply=%region_11.12 | all-reduce | flops 6 | bytes 48 | tf_op jit(solution)/shard_map/psum | solution.py:61
  177.7 5.3 %convolution_convert_fusion.2 = bf16[2048,768]{1,0:T(8,128)(2,1)} fusion(bf16[2048,768]{1,0:T(8,128)(2,1)S(1)} %fusion.11, bf16[768,3072]{1,0:T(8,128)(2,1)} %all-gather.2.cloned.1.call-done), kind=kOutput, calls=%fused_computation.41 | convolution fusion | flops 2417491968 | bytes 7471104 | tf_op jit(solution)/shard_map/dot_general | solution.py:74
  182.9 4.7 %copy.27 = bf16[2048,768]{0,1:T(8,128)(2,1)} copy(bf16[2048,768]{1,0:T(8,128)(2,1)} %convolution_convert_fusion.2) | data formatting | bytes 6291456 | tf_op jit(solution)/shard_map/convert_element_type | solution.py:75
  192.2 9.0 %convert_bitcast_fusion.2 = bf16[16,128,1,12,64]{1,4,3,0,2:T(8,128)(2,1)} fusion(bf16[16,12,128,128]{2,3,1,0:T(8,128)(2,1)} %copy-done.2, bf16[16,12,64,128]{3,0,2,1:T(8,128)(2,1)S(1)} %bitcast.108), kind=kOutput, calls=%fused_computation.50 | convolution fusion | flops 404226048 | bytes 12582912 | tf_op jit(solution)/shard_map/transpose(jvp(bhqk,bkhd->bqhd))/dot_general | solution.py:29
  201.2 12.6 %fusion.3 = (f32[16,12,128]{2,1,0:T(8,128)S(1)}, bf16[16,12,128,128]{2,3,1,0:T(8,128)(2,1)}) fusion(f32[16,12,128]{2,1,0:T(8,128)S(1)} %multiply_divide_fusion, f32[16,12,128]{2,1,0:T(8,128)S(1)} %get-tuple-element.20, f32[16,12,128,128]{2,3,1,0:T(8,128)} %copy-done, f32[12,128,128]{1,2,0:T(8,128)S(1)} %copy-done.11, ...), kind=kOutput, calls=%fused_computation.5 | convolution fusion | flops 427794432 | bytes 26249216 | tf_op jit(solution)/shard_map/transpose(jvp(bhqk,bkhd->bqhd))/dot_general | solution.py:29
  213.9 10.1 %fusion.53 = (f32[16,12,128]{2,1,0:T(8,128)S(1)}, f32[16,12,128,128]{2,3,1,0:T(8,128)}) fusion(f32[16,12,128]{2,1,0:T(8,128)S(1)} %get-tuple-element.20, f32[16,12,128,128]{2,3,1,0:T(8,128)S(1)} %bitcast.102, f32[12,128,128]{1,2,0:T(8,128)S(1)} %copy-done.11, pred[16,128]{1,0:T(8,128)(4,1)S(1)} %iota_compare_fusion, f32[16,12,128]{2,1,0:T(8,128)S(1)} %neg.9, ...), kind=kLoop, calls=%fused_computation.90 | loop fusion | flops 25141248 | bytes 32638976 | tf_op jit(solution)/shard_map/transpose(jvp())/reduce_sum | solution.py:27
  224.1 11.4 %convert_bitcast_fusion.1 = bf16[16,128,1,12,64]{1,4,3,0,2:T(8,128)(2,1)} fusion(bf16[16,128,1,12,64]{1,0,4,3,2:T(8,128)(2,1)} %get-tuple-element.14, f32[16,12,128,128]{2,3,1,0:T(8,128)} %get-tuple-element.9, pred[16,12,128,128]{2,3,1,0:T(32,128)(4,1)} %get-tuple-element.11, f32[16,12,128]{2,1,0:T(8,128)S(1)} %negate_divide_fusion, ...), kind=kOutput, calls=%fused_computation.49 | convolution fusion | flops 413663232 | bytes 22120448 | tf_op jit(solution)/shard_map/transpose(jvp(bqhd,bkhd->bhqk))/dot_general | solution.py:20
  237.0 4.2 convert_bitcast_fusion
  244.2 6.8 %pad_add_fusion = bf16[16,128,3,12,64]{1,4,3,0,2:T(8,128)(2,1)} fusion(bf16[16,128,1,12,64]{1,4,3,0,2:T(8,128)(2,1)} %convert_bitcast_fusion, bf16[16,128,1,12,64]{1,4,3,0,2:T(8,128)(2,1)} %convert_bitcast_fusion.1, bf16[16,128,1,12,64]{1,4,3,0,2:T(8,128)(2,1)S(1)} %copy-done.12), kind=kLoop, calls=%fused_computation.17 | loop fusion | flops 9437184 | bytes 18874368 | tf_op jit(solution)/shard_map/transpose(jvp())/add_any | solution.py:21
  251.0 26.1 %copy.33 = bf16[16,128,3,12,64]{1,0,4,3,2:T(8,128)(2,1)} copy(bf16[16,128,3,12,64]{1,4,3,0,2:T(8,128)(2,1)} %pad_add_fusion) | data formatting | bytes 18874368 | tf_op jit(solution)/shard_map/transpose(jvp())/add_any | solution.py:21
  279.6 11.4 %fusion.22 = bf16[768,2304]{1,0:T(8,128)(2,1)S(1)} fusion(bf16[2048,768]{1,0:T(8,128)(2,1)S(1)} %bitcast.113, bf16[288,8,16,128]{3,2,1,0:T(8,128)(2,1)} %bitcast.110), kind=kOutput, calls=%fused_computation.37 | convolution fusion | flops 7249526784 | bytes 16121856 | tf_op jit(solution)/shard_map/dot_general | solution.py:78
  296.5 94.1 %reduce-scatter.2.cloned.1.call-done = bf16[96,3072]{1,0:T(8,128)(2,1)} async-done(((bf16[768,3072]{1,0:T(8,128)(2,1)}), bf16[96,3072]{1,0:T(8,128)(2,1)}) %reduce-scatter.2.cloned.1.call-update) | async-done | bytes 589840 | tf_op jit(solution)/shard_map/reduce_scatter | solution.py:80
  390.6 35.8 %all-reduce.6.cloned.1.call-done = bf16[96,3072]{1,0:T(8,128)(2,1)} async-done(((bf16[96,3072]{1,0:T(8,128)(2,1)}), bf16[96,3072]{1,0:T(8,128)(2,1)}) %all-reduce.6.cloned.1.call-update) | async-done | bytes 589840 | tf_op jit(solution)/shard_map/psum | solution.py:86
  428.9 22.0 %psum.38 = f32[]{:T(128)} all-reduce(f32[]{:T(128)} %fusion.41), channel_id=1, replica_groups=mesh['dp'=8,'cand'=4] {'dp'}, use_global_device_ids=true, to_apply=%region_19.20 | all-reduce | flops 1 | bytes 8 | tf_op jit(solution)/shard_map/psum | solution.py:87
  (84 shorter events, 40.2 us)
Async XLA Ops:
  7.2 6.8 %copy-start.5 = (bf16[2,8,128,768]{3,2,1,0:T(8,128)(2,1)S(1)}, bf16[2,8,128,768]{3,2,1,0:T(8,128)(2,1)}, u32[]{:S(2)}) copy-start(bf16[2,8,128,768]{3,2,1,0:T(8,128)(2,1)} %param.7) | copy-start | bytes 9437188
  7.2 6.8 %copy-start.17 = (f32[768]{0:T(1024)S(1)}, f32[768]{0:T(1024)}, u32[]{:S(2)}) copy-start(f32[768]{0:T(1024)} %param.9) | copy-start | bytes 9220
  7.2 85.1 %all-gather.2.cloned.1.call-start = ((), (), s32[]{:S(2)}) async-start(), calls=%async_computation.1 | async-start | bytes 5308416 | tf_op jit(solution)/shard_map/all_gather | solution.py:41
  7.9 382.7 %reduce-scatter.2.cloned.1.call-start = ((), (), s32[]{:S(2)}) async-start(), calls=%async_computation.2 | async-start | bytes 5308416 | tf_op jit(solution)/shard_map/reduce_scatter | solution.py:80
  128.4 6.4 %copy-start.11 = (f32[12,128,128]{1,2,0:T(8,128)S(1)}, f32[12,128,128]{1,2,0:T(8,128)}, u32[]{:S(2)}) copy-start(f32[12,128,128]{1,2,0:T(8,128)} %copy.24) | copy-start | bytes 2359300
  134.8 7.6 %copy-start.3 = (bf16[16,128,1,12,64]{1,0,4,3,2:T(8,128)(2,1)}, bf16[16,128,1,12,64]{1,0,4,3,2:T(8,128)(2,1)S(1)}, u32[]{:S(2)}) copy-start(bf16[16,128,1,12,64]{1,0,4,3,2:T(8,128)(2,1)S(1)} %get-tuple-element.15) | copy-start | bytes 9437188
  142.3 4.6 copy-start
  146.9 8.1 %copy-start.8 = (bf16[16,128,1,12,64]{1,0,4,3,2:T(8,128)(2,1)S(1)}, bf16[16,128,1,12,64]{1,0,4,3,2:T(8,128)(2,1)}, u32[]{:S(2)}) copy-start(bf16[16,128,1,12,64]{1,0,4,3,2:T(8,128)(2,1)} %get-tuple-element.13) | copy-start | bytes 9437188
  155.0 3.2 copy-start.2
  155.0 4.2 copy-start.6
  158.2 5.6 %copy-start.9 = (bf16[16,12,64,128]{3,2,1,0:T(8,128)(2,1)}, bf16[16,12,64,128]{3,2,1,0:T(8,128)(2,1)S(1)}, u32[]{:S(2)}) copy-start(bf16[16,12,64,128]{3,2,1,0:T(8,128)(2,1)S(1)} %fusion.36) | copy-start | bytes 9437188
  159.2 4.7 %copy-start.16 = (f32[768]{0:T(1024)S(1)}, f32[768]{0:T(1024)}, u32[]{:S(2)}) copy-start(f32[768]{0:T(1024)} %param.11) | copy-start | bytes 9220
  159.2 10.8 %copy-start.18 = (s32[2,8]{1,0:T(2,128)S(1)}, s32[2,8]{1,0:T(2,128)}, u32[]{:S(2)}) copy-start(s32[2,8]{1,0:T(2,128)} %param.13) | copy-start | bytes 196
  192.2 21.7 %slice-start = ((s8[12582912]{0:T(1024)(128)(4,1)}), s8[4194304]{0:T(1024)(128)(4,1)S(1)}, s32[]{:S(2)}) async-start(s8[12582912]{0:T(1024)(128)(4,1)} %bitcast.101), calls=%async_computation.4 | async-start | bytes 8388608
  201.2 12.7 %slice-start.1 = ((s8[12582912]{0:T(1024)(128)(4,1)}), s8[4194304]{0:T(1024)(128)(4,1)S(1)}, s32[]{:S(2)}) async-start(s8[12582912]{0:T(1024)(128)(4,1)} %bitcast.101), calls=%async_computation.5 | async-start | bytes 8388608
  201.2 12.7 %slice-start.2 = ((s8[12582912]{0:T(1024)(128)(4,1)}), s8[4194304]{0:T(1024)(128)(4,1)S(1)}, s32[]{:S(2)}) async-start(s8[12582912]{0:T(1024)(128)(4,1)} %bitcast.101), calls=%async_computation.6 | async-start | bytes 8388608
  224.1 11.4 %copy-start.1 = (f32[16,12,128,128]{2,3,1,0:T(8,128)S(1)}, f32[16,12,128,128]{2,3,1,0:T(8,128)}, u32[]{:S(2)}) copy-start(f32[16,12,128,128]{2,3,1,0:T(8,128)} %get-tuple-element.9) | copy-start | bytes 37748740
  224.1 11.8 %copy-start.4 = (bf16[16,128,1,12,64]{1,0,4,3,2:T(8,128)(2,1)S(1)}, bf16[16,128,1,12,64]{1,0,4,3,2:T(8,128)(2,1)}, u32[]{:S(2)}) copy-start(bf16[16,128,1,12,64]{1,0,4,3,2:T(8,128)(2,1)} %copy-done.3) | copy-start | bytes 9437188
  224.1 12.9 %copy-start.7 = (pred[16,12,128,128]{2,3,1,0:T(32,128)(4,1)S(1)}, pred[16,12,128,128]{2,3,1,0:T(32,128)(4,1)}, u32[]{:S(2)}) copy-start(pred[16,12,128,128]{2,3,1,0:T(32,128)(4,1)} %get-tuple-element.11) | copy-start | bytes 9437188
  241.2 3.0 copy-start.12
  251.0 26.2 %copy-start.10 = (bf16[16,12,64,128]{3,2,1,0:T(8,128)(2,1)S(1)}, bf16[16,12,64,128]{3,2,1,0:T(8,128)(2,1)}, u32[]{:S(2)}) copy-start(bf16[16,12,64,128]{3,2,1,0:T(8,128)(2,1)} %copy-done.9) | copy-start | bytes 9437188
  277.2 2.5 copy-start.15
  279.6 11.4 %copy-start.14 = (bf16[16,128,768]{2,1,0:T(8,128)(2,1)S(1)}, bf16[16,128,768]{2,1,0:T(8,128)(2,1)}, u32[]{:S(2)}) copy-start(bf16[16,128,768]{2,1,0:T(8,128)(2,1)} %multiply_convert_fusion) | copy-start | bytes 9437188
  296.5 130.0 %all-reduce.6.cloned.1.call-start = ((), (), s32[]{:S(2)}) async-start(), calls=%async_computation.3 | async-start | bytes 1179648 | tf_op jit(solution)/shard_map/psum | solution.py:86
  (1 other events, 1.6 us)
Sparse Core Ops, SparseCore 0:
  10.2 82.0 all-gather.1
  296.6 93.9 reduce-scatter.1
  393.0 33.3 all-reduce.5
where the time goes:
time: 464 us; the launch traced here: 461 us
  waiting for transfers between devices  204 us (44%)
  matrix products  83.9 us (18%)
  local copies, waits for them, and re-layouts  76.2 us (16%)
  other arithmetic  47.1 us (10%)
  blocking collectives  34.2 us (7%)
  between operations  15.2 us (3%)
    reduce_scatter x1, waiting for transfers between devices, shards(): lax.psum_scatter(jnp.concatenate([first, second], axis=1).astype(jnp.bflo...  94.1 us
    all_gather x1, waiting for transfers between devices, shards(): weights = lax.all_gather(attn_weight, 'dp', axis=0, tiled=True)  73.4 us
    psum x1, waiting for transfers between devices, shards(): shard = lax.psum(shard.astype(jnp.bfloat16), 'cand').astype(jnp.float32)  35.8 us
    add_any x1, local copies, waits for them, and re-layouts, attend(): parts[:, :, 0]  26.1 us
    dot_general x3, matrix products, attend(): jnp.einsum('bhqk,bkhd->bqhd', probs, parts[:, :, 2], preferred_element_ty...  24.4 us
    dot_general x3, matrix products, attend(): jnp.einsum('bqhd,bkhd->bhqk', parts[:, :, 0], parts[:, :, 1], preferred_e...  23.1 us
    unnamed x47, local copies, waits for them, and re-layouts  22.7 us
    psum x1, blocking collectives, shards(): squares = lax.psum(jnp.sum(shard * shard), 'dp')  22 us
  transfers between devices with their start and end apart: 3, of which 3 were waited for; matrix products, arithmetic and copies ran while one was open for 2% of the time, Pallas kernels for 0%

commit v1 on v0

--- a/solution.py
+++ b/solution.py
@@ -4,6 +4,11 @@
 from jax.sharding import PartitionSpec as P
 
 EPS = 1e-06
+
+
+def summed_here(x, name):
+    parts = lax.all_gather(x, name)
+    return jnp.sum(parts, axis=0)
 
 
 def rms_rows(values, gain):
@@ -83,7 +88,7 @@
         scatter_dimension=0,
         tiled=True,
     ).astype(jnp.float32)
-    shard = lax.psum(shard.astype(jnp.bfloat16), "cand").astype(jnp.float32)
+    shard = summed_here(shard.astype(jnp.bfloat16), "cand").astype(jnp.float32)
     squares = lax.psum(jnp.sum(shard * shard), "dp")
     rms_value = jnp.sqrt(squares / (4.0 * width * width))
     update = shard / (rms_value + EPS)

time: 464 us -> 454 us (0.978)
  waiting for transfers between devices: 204 us -> 194 us
    psum x1 -> x0, waiting for transfers between devices: 35.8 us -> none  [shards(): shard = lax.psum(shard.astype(jnp.bfloat16), 'cand').astype(jnp.float32)]
    all_gather x0 -> x1, waiting for transfers between devices: none -> 25.3 us  [summed_here(): parts = lax.all_gather(x, name)]
where the time goes in v1:
time: 454 us; the launch traced here: 450 us
  waiting for transfers between devices  194 us (43%)
  matrix products  83.9 us (18%)
  local copies, waits for them, and re-layouts  76.2 us (17%)
  other arithmetic  47.1 us (10%)
  blocking collectives  34.2 us (8%)
  between operations  15.2 us (3%)
    reduce_scatter x1, waiting for transfers between devices, shards(): lax.psum_scatter(jnp.concatenate([first, second], axis=1).astype(jnp.bflo...  94.1 us
    all_gather x1, waiting for transfers between devices, shards(): weights = lax.all_gather(attn_weight, 'dp', axis=0, tiled=True)  73.4 us
    add_any x1, local copies, waits for them, and re-layouts, attend(): parts[:, :, 0]  26.1 us
    all_gather x1, waiting for transfers between devices, summed_here(): parts = lax.all_gather(x, name)  25.3 us
    dot_general x3, matrix products, attend(): jnp.einsum('bhqk,bkhd->bqhd', probs, parts[:, :, 2], preferred_element_ty...  24.4 us
    dot_general x3, matrix products, attend(): jnp.einsum('bqhd,bkhd->bhqk', parts[:, :, 0], parts[:, :, 1], preferred_e...  23.1 us
    unnamed x47, local copies, waits for them, and re-layouts  22.7 us
    psum x1, blocking collectives, shards(): squares = lax.psum(jnp.sum(shard * shard), 'dp')  22 us
  transfers between devices with their start and end apart: 3, of which 3 were waited for; matrix products, arithmetic and copies ran while one was open for 2% of the time, Pallas kernels for 0%

profile of v1, /device:TPU:0, one launch (start us, length us, event | category | flops | bytes accessed | tf_op | source)
XLA Modules:
  0.0 450.2 jit_solution(3799032806727815553)
XLA Ops:
  18.8 73.4 %all-gather.4.cloned.1.call-done = bf16[768,3072]{1,0:T(8,128)(2,1)} async-done(((bf16[96,3072]{1,0:T(8,128)(2,1)}), bf16[768,3072]{1,0:T(8,128)(2,1)}) %all-gather.4.cloned.1.call-update) | async-done | bytes 4718608 | tf_op jit(solution)/shard_map/all_gather | solution.py:46
  92.3 12.5 %convolution_convert_fusion = bf16[2048,2304]{1,0:T(8,128)(2,1)} fusion(bf16[2048,768]{1,0:T(8,128)(2,1)} %fusion.13, bf16[768,3072]{1,0:T(8,128)(2,1)} %all-gather.4.cloned.1.call-done), kind=kOutput, calls=%fused_computation.11 | convolution fusion | flops 7252475904 | bytes 16121856 | tf_op jit(solution)/shard_map/dot_general | solution.py:52
  104.8 12.7 %copy.20 = bf16[2048,2304]{0,1:T(8,128)(2,1)} copy(bf16[2048,2304]{1,0:T(8,128)(2,1)} %convolution_convert_fusion) | data formatting | bytes 18874368 | tf_op jit(solution)/shard_map/convert_element_type | solution.py:53
  117.5 10.9 %copy.45 = bf16[288,8,16,128]{3,2,1,0:T(8,128)(2,1)} copy(bf16[288,8,16,128]{3,1,2,0:T(8,128)(2,1)} %bitcast.105) | data formatting | bytes 18874368
  128.4 6.4 %fusion.56 = (bf16[16,128,1,12,64]{1,0,4,3,2:T(8,128)(2,1)}, bf16[16,128,1,12,64]{1,0,4,3,2:T(8,128)(2,1)}, bf16[16,128,1,12,64]{1,0,4,3,2:T(8,128)(2,1)S(1)}) fusion(bf16[16,128,3,12,64]{1,0,4,3,2:T(8,128)(2,1)} %bitcast.104), kind=kLoop, calls=%fused_computation.91 | loop fusion | bytes 18874368 | tf_op jit(solution)/shard_map/jvp()/slice | solution.py:35
  134.8 7.5 %fusion.5 = (f32[16,12,128]{2,1,0:T(8,128)S(1)}, f32[16,12,128,128]{2,3,1,0:T(8,128)S(1)}) fusion(f32[12,128,128]{1,2,0:T(8,128)S(1)} %copy-done.11, pred[16,128]{1,0:T(8,128)(4,1)S(1)} %iota_compare_fusion, bf16[16,128,1,12,64]{1,0,4,3,2:T(8,128)(2,1)S(1)} %get-tuple-element.15, bf16[16,128,1,12,64]{1,0,4,3,2:T(8,128)(2,1)} %get-tuple-element.14), kind=kOutput, calls=%fused_computation.13 | convolution fusion | flops 412065792 | bytes 19761152 | tf_op jit(solution)/shard_map/jvp(bqhd,bkhd->bhqk)/dot_general | solution.py:25
  142.3 3.4 fusion.37
  146.9 8.1 %convert_reduce_fusion = (f32[16,12,128]{2,1,0:T(8,128)S(1)}, pred[16,12,128,128]{2,3,1,0:T(32,128)(4,1)}, bf16[16,12,128,128]{2,3,1,0:T(8,128)(2,1)S(1)}) fusion(f32[16,12,128]{2,1,0:T(8,128)S(1)} %get-tuple-element.20, f32[16,12,128,128]{2,3,1,0:T(8,128)S(1)} %get-tuple-element.21, f32[12,128,128]{1,2,0:T(8,128)S(1)} %copy-done.11, ...), kind=kLoop, calls=%fused_computation.7 | loop fusion | flops 25141248 | bytes 23103488 | tf_op jit(solution)/shard_map/jvp()/reduce_sum | solution.py:31
  159.2 4.6 %fusion.15 = f32[16,768]{1,0:T(8,128)S(1)} fusion(f32[16,128]{1,0:T(8,128)S(1)} %get-tuple-element.19, bf16[2,8,128,768]{3,2,1,0:T(8,128)(2,1)S(1)} %copy-done.6, bf16[16,128,768]{1,2,0:T(8,128)(2,1)S(1)} %bitcast.106, bf16[768,3072]{1,0:T(8,128)(2,1)} %all-gather.4.cloned.1.call-done), kind=kOutput, calls=%fused_computation.27 | convolution fusion | flops 2422198272 | bytes 7528448 | tf_op jit(solution)/shard_map/dot_general | solution.py:56
  164.3 5.7 %pmax.7 = f32[2]{0:T(128)S(1)} all-reduce(f32[2]{0:T(128)S(1)} %reduce_max.19), channel_id=1, replica_groups=mesh['dp'=8,'cand'=4] {'cand'}, use_global_device_ids=true, to_apply=%region_7.8 | all-reduce | flops 2 | bytes 16 | tf_op jit(solution)/shard_map/pmax | solution.py:65
  170.2 6.6 %all-reduce.3 = (f32[2]{0:T(128)S(1)}, f32[2]{0:T(128)S(1)}, f32[2]{0:T(128)S(1)}) all-reduce(f32[2]{0:T(128)S(1)} %get-tuple-element.3, f32[2]{0:T(128)S(1)} %get-tuple-element.4, f32[2]{0:T(128)S(1)} %get-tuple-element.2), channel_id=1, replica_groups=mesh['dp'=8,'cand'=4] {'cand'}, use_global_device_ids=true, to_apply=%region_11.12 | all-reduce | flops 6 | bytes 48 | tf_op jit(solution)/shard_map/psum | solution.py:66
  177.7 5.3 %convolution_convert_fusion.2 = bf16[2048,768]{1,0:T(8,128)(2,1)} fusion(bf16[2048,768]{1,0:T(8,128)(2,1)S(1)} %fusion.11, bf16[768,3072]{1,0:T(8,128)(2,1)} %all-gather.4.cloned.1.call-done), kind=kOutput, calls=%fused_computation.41 | convolution fusion | flops 2417491968 | bytes 7471104 | tf_op jit(solution)/shard_map/dot_general | solution.py:79
  182.9 4.7 %copy.27 = bf16[2048,768]{0,1:T(8,128)(2,1)} copy(bf16[2048,768]{1,0:T(8,128)(2,1)} %convolution_convert_fusion.2) | data formatting | bytes 6291456 | tf_op jit(solution)/shard_map/convert_element_type | solution.py:80
  192.2 9.0 %convert_bitcast_fusion.2 = bf16[16,128,1,12,64]{1,4,3,0,2:T(8,128)(2,1)} fusion(bf16[16,12,128,128]{2,3,1,0:T(8,128)(2,1)} %copy-done.2, bf16[16,12,64,128]{3,0,2,1:T(8,128)(2,1)S(1)} %bitcast.109), kind=kOutput, calls=%fused_computation.50 | convolution fusion | flops 404226048 | bytes 12582912 | tf_op jit(solution)/shard_map/transpose(jvp(bhqk,bkhd->bqhd))/dot_general | solution.py:34
  201.2 12.6 %fusion.3 = (f32[16,12,128]{2,1,0:T(8,128)S(1)}, bf16[16,12,128,128]{2,3,1,0:T(8,128)(2,1)}) fusion(f32[16,12,128]{2,1,0:T(8,128)S(1)} %multiply_divide_fusion, f32[16,12,128]{2,1,0:T(8,128)S(1)} %get-tuple-element.20, f32[16,12,128,128]{2,3,1,0:T(8,128)} %copy-done, f32[12,128,128]{1,2,0:T(8,128)S(1)} %copy-done.11, ...), kind=kOutput, calls=%fused_computation.5 | convolution fusion | flops 427794432 | bytes 26249216 | tf_op jit(solution)/shard_map/transpose(jvp(bhqk,bkhd->bqhd))/dot_general | solution.py:34
  213.9 10.1 %fusion.53 = (f32[16,12,128]{2,1,0:T(8,128)S(1)}, f32[16,12,128,128]{2,3,1,0:T(8,128)}) fusion(f32[16,12,128]{2,1,0:T(8,128)S(1)} %get-tuple-element.20, f32[16,12,128,128]{2,3,1,0:T(8,128)S(1)} %bitcast.103, f32[12,128,128]{1,2,0:T(8,128)S(1)} %copy-done.11, pred[16,128]{1,0:T(8,128)(4,1)S(1)} %iota_compare_fusion, f32[16,12,128]{2,1,0:T(8,128)S(1)} %neg.9, ...), kind=kLoop, calls=%fused_computation.90 | loop fusion | flops 25141248 | bytes 32638976 | tf_op jit(solution)/shard_map/transpose(jvp())/reduce_sum | solution.py:32
  224.1 11.4 %convert_bitcast_fusion.1 = bf16[16,128,1,12,64]{1,4,3,0,2:T(8,128)(2,1)} fusion(bf16[16,128,1,12,64]{1,0,4,3,2:T(8,128)(2,1)} %get-tuple-element.14, f32[16,12,128,128]{2,3,1,0:T(8,128)} %get-tuple-element.9, pred[16,12,128,128]{2,3,1,0:T(32,128)(4,1)} %get-tuple-element.11, f32[16,12,128]{2,1,0:T(8,128)S(1)} %negate_divide_fusion, ...), kind=kOutput, calls=%fused_computation.49 | convolution fusion | flops 413663232 | bytes 22120448 | tf_op jit(solution)/shard_map/transpose(jvp(bqhd,bkhd->bhqk))/dot_general | solution.py:25
  237.0 4.2 convert_bitcast_fusion
  244.2 6.8 %pad_add_fusion = bf16[16,128,3,12,64]{1,4,3,0,2:T(8,128)(2,1)} fusion(bf16[16,128,1,12,64]{1,4,3,0,2:T(8,128)(2,1)} %convert_bitcast_fusion, bf16[16,128,1,12,64]{1,4,3,0,2:T(8,128)(2,1)} %convert_bitcast_fusion.1, bf16[16,128,1,12,64]{1,4,3,0,2:T(8,128)(2,1)S(1)} %copy-done.12), kind=kLoop, calls=%fused_computation.17 | loop fusion | flops 9437184 | bytes 18874368 | tf_op jit(solution)/shard_map/transpose(jvp())/add_any | solution.py:26
  251.0 26.1 %copy.33 = bf16[16,128,3,12,64]{1,0,4,3,2:T(8,128)(2,1)} copy(bf16[16,128,3,12,64]{1,4,3,0,2:T(8,128)(2,1)} %pad_add_fusion) | data formatting | bytes 18874368 | tf_op jit(solution)/shard_map/transpose(jvp())/add_any | solution.py:26
  279.6 11.4 %fusion.22 = bf16[768,2304]{1,0:T(8,128)(2,1)S(1)} fusion(bf16[2048,768]{1,0:T(8,128)(2,1)S(1)} %bitcast.114, bf16[288,8,16,128]{3,2,1,0:T(8,128)(2,1)} %bitcast.111), kind=kOutput, calls=%fused_computation.37 | convolution fusion | flops 7249526784 | bytes 16121856 | tf_op jit(solution)/shard_map/dot_general | solution.py:83
  296.5 94.1 %reduce-scatter.2.cloned.1.call-done = bf16[96,3072]{1,0:T(8,128)(2,1)} async-done(((bf16[768,3072]{1,0:T(8,128)(2,1)}), bf16[96,3072]{1,0:T(8,128)(2,1)}) %reduce-scatter.2.cloned.1.call-update) | async-done | bytes 589840 | tf_op jit(solution)/shard_map/reduce_scatter | solution.py:85
  390.6 25.3 %all-gather.6.cloned.1.call-done = bf16[384,3072]{1,0:T(8,128)(2,1)} async-done(((bf16[96,3072]{1,0:T(8,128)(2,1)}), bf16[384,3072]{1,0:T(8,128)(2,1)}) %all-gather.6.cloned.1.call-update) | async-done | bytes 2359312 | tf_op jit(solution)/shard_map/all_gather | solution.py:10
  419.4 22.0 %psum.30 = f32[]{:T(128)} all-reduce(f32[]{:T(128)} %fusion.41), channel_id=1, replica_groups=mesh['dp'=8,'cand'=4] {'dp'}, use_global_device_ids=true, to_apply=%region_19.20 | all-reduce | flops 1 | bytes 8 | tf_op jit(solution)/shard_map/psum | solution.py:92
  (85 shorter events, 40.2 us)
Async XLA Ops:
  7.2 6.8 %copy-start.5 = (bf16[2,8,128,768]{3,2,1,0:T(8,128)(2,1)S(1)}, bf16[2,8,128,768]{3,2,1,0:T(8,128)(2,1)}, u32[]{:S(2)}) copy-start(bf16[2,8,128,768]{3,2,1,0:T(8,128)(2,1)} %param.7) | copy-start | bytes 9437188
  7.2 6.8 %copy-start.17 = (f32[768]{0:T(1024)S(1)}, f32[768]{0:T(1024)}, u32[]{:S(2)}) copy-start(f32[768]{0:T(1024)} %param.9) | copy-start | bytes 9220
  7.2 85.1 %all-gather.4.cloned.1.call-start = ((), (), s32[]{:S(2)}) async-start(), calls=%async_computation.1 | async-start | bytes 5308416 | tf_op jit(solution)/shard_map/all_gather | solution.py:46
  7.9 382.7 %reduce-scatter.2.cloned.1.call-start = ((), (), s32[]{:S(2)}) async-start(), calls=%async_computation.2 | async-start | bytes 5308416 | tf_op jit(solution)/shard_map/reduce_scatter | solution.py:85
  128.4 6.4 %copy-start.11 = (f32[12,128,128]{1,2,0:T(8,128)S(1)}, f32[12,128,128]{1,2,0:T(8,128)}, u32[]{:S(2)}) copy-start(f32[12,128,128]{1,2,0:T(8,128)} %copy.24) | copy-start | bytes 2359300
  134.8 7.6 %copy-start.3 = (bf16[16,128,1,12,64]{1,0,4,3,2:T(8,128)(2,1)}, bf16[16,128,1,12,64]{1,0,4,3,2:T(8,128)(2,1)S(1)}, u32[]{:S(2)}) copy-start(bf16[16,128,1,12,64]{1,0,4,3,2:T(8,128)(2,1)S(1)} %get-tuple-element.15) | copy-start | bytes 9437188
  142.3 4.6 %copy-start = (f32[16,12,128,128]{2,3,1,0:T(8,128)}, f32[16,12,128,128]{2,3,1,0:T(8,128)S(1)}, u32[]{:S(2)}) copy-start(f32[16,12,128,128]{2,3,1,0:T(8,128)S(1)} %get-tuple-element.21) | copy-start | bytes 37748740
  146.9 8.1 %copy-start.8 = (bf16[16,128,1,12,64]{1,0,4,3,2:T(8,128)(2,1)S(1)}, bf16[16,128,1,12,64]{1,0,4,3,2:T(8,128)(2,1)}, u32[]{:S(2)}) copy-start(bf16[16,128,1,12,64]{1,0,4,3,2:T(8,128)(2,1)} %get-tuple-element.13) | copy-start | bytes 9437188
  155.0 3.2 copy-start.2
  155.0 4.2 copy-start.6
  158.2 5.6 %copy-start.9 = (bf16[16,12,64,128]{3,2,1,0:T(8,128)(2,1)}, bf16[16,12,64,128]{3,2,1,0:T(8,128)(2,1)S(1)}, u32[]{:S(2)}) copy-start(bf16[16,12,64,128]{3,2,1,0:T(8,128)(2,1)S(1)} %fusion.36) | copy-start | bytes 9437188
  159.2 4.7 %copy-start.16 = (f32[768]{0:T(1024)S(1)}, f32[768]{0:T(1024)}, u32[]{:S(2)}) copy-start(f32[768]{0:T(1024)} %param.11) | copy-start | bytes 9220
  159.2 10.8 %copy-start.18 = (s32[2,8]{1,0:T(2,128)S(1)}, s32[2,8]{1,0:T(2,128)}, u32[]{:S(2)}) copy-start(s32[2,8]{1,0:T(2,128)} %param.13) | copy-start | bytes 196
  192.2 21.7 %slice-start = ((s8[12582912]{0:T(1024)(128)(4,1)}), s8[4194304]{0:T(1024)(128)(4,1)S(1)}, s32[]{:S(2)}) async-start(s8[12582912]{0:T(1024)(128)(4,1)} %bitcast.102), calls=%async_computation.4 | async-start | bytes 8388608
  201.2 12.7 %slice-start.1 = ((s8[12582912]{0:T(1024)(128)(4,1)}), s8[4194304]{0:T(1024)(128)(4,1)S(1)}, s32[]{:S(2)}) async-start(s8[12582912]{0:T(1024)(128)(4,1)} %bitcast.102), calls=%async_computation.5 | async-start | bytes 8388608
  201.2 12.7 %slice-start.2 = ((s8[12582912]{0:T(1024)(128)(4,1)}), s8[4194304]{0:T(1024)(128)(4,1)S(1)}, s32[]{:S(2)}) async-start(s8[12582912]{0:T(1024)(128)(4,1)} %bitcast.102), calls=%async_computation.6 | async-start | bytes 8388608
  224.1 11.4 %copy-start.1 = (f32[16,12,128,128]{2,3,1,0:T(8,128)S(1)}, f32[16,12,128,128]{2,3,1,0:T(8,128)}, u32[]{:S(2)}) copy-start(f32[16,12,128,128]{2,3,1,0:T(8,128)} %get-tuple-element.9) | copy-start | bytes 37748740
  224.1 11.8 %copy-start.4 = (bf16[16,128,1,12,64]{1,0,4,3,2:T(8,128)(2,1)S(1)}, bf16[16,128,1,12,64]{1,0,4,3,2:T(8,128)(2,1)}, u32[]{:S(2)}) copy-start(bf16[16,128,1,12,64]{1,0,4,3,2:T(8,128)(2,1)} %copy-done.3) | copy-start | bytes 9437188
  224.1 12.9 %copy-start.7 = (pred[16,12,128,128]{2,3,1,0:T(32,128)(4,1)S(1)}, pred[16,12,128,128]{2,3,1,0:T(32,128)(4,1)}, u32[]{:S(2)}) copy-start(pred[16,12,128,128]{2,3,1,0:T(32,128)(4,1)} %get-tuple-element.11) | copy-start | bytes 9437188
  241.2 3.0 copy-start.12
  251.0 26.2 %copy-start.10 = (bf16[16,12,64,128]{3,2,1,0:T(8,128)(2,1)S(1)}, bf16[16,12,64,128]{3,2,1,0:T(8,128)(2,1)}, u32[]{:S(2)}) copy-start(bf16[16,12,64,128]{3,2,1,0:T(8,128)(2,1)} %copy-done.9) | copy-start | bytes 9437188
  277.2 2.5 copy-start.15
  279.6 11.4 %copy-start.14 = (bf16[16,128,768]{2,1,0:T(8,128)(2,1)S(1)}, bf16[16,128,768]{2,1,0:T(8,128)(2,1)}, u32[]{:S(2)}) copy-start(bf16[16,128,768]{2,1,0:T(8,128)(2,1)} %multiply_convert_fusion) | copy-start | bytes 9437188
  296.5 119.5 %all-gather.6.cloned.1.call-start = ((), (), s32[]{:S(2)}) async-start(), calls=%async_computation.3 | async-start | bytes 2949120 | tf_op jit(solution)/shard_map/all_gather | solution.py:10
  (1 other events, 1.6 us)
Sparse Core Ops, SparseCore 0:
  10.2 82.0 all-gather.3
  296.6 93.9 reduce-scatter.1
  392.2 23.6 all-gather.5
